TPU v7x, 32 devices: a whole 2x2x4 slice. The times are simulated.
32 devices in a mesh: img: 8 (over z, x), row: 4 (over y, core).
Axes of the slice: x: 2, y: 2, z: 4, core: 2. Of those that a mesh axis runs over, the one named last changes fastest.
Arguments:
- tokens: bfloat16 [8, 32, 128, 1024], P('img', 'row'), may hold values from -14 to 14
- proj_weight: bfloat16 [1024, 256], replicated, may hold values from -0.1875 to 0.1875
- proj_bias: float32 [256], replicated, may hold values from -3 to 3
- conv_weight: bfloat16 [4, 3, 3, 256, 256], replicated, may hold values from -0.125 to 0.125
- bn_gain: float32 [4, 256], replicated, may hold values from 0.1 to 1.9
- bn_bias: float32 [4, 256], replicated, may hold values from -3 to 3
Outputs:
- joining_out: bfloat16 [8, 32, 128, 256], P('img', 'row')
All inputs are finite; a program needn't handle non-finite values.
Results may differ from a plain program's by a relative error of at most 0.0071.
Values may be sent and summed in bfloat16 or wider, within the bound.
A program may use at most 64 MiB of HBM per device.

v0:
```python
import jax
import jax.numpy as jnp
from jax import lax
from jax.sharding import PartitionSpec as P

epsilon = 1e-05


def extended(value, sides, width):
    for axis, dim in sides:
        devices, length = (lax.axis_size(axis), value.shape[dim])
        up = [(i, (i + 1) % devices) for i in range(devices - 1)]
        down = [(j, i) for i, j in up]
        last = lax.slice_in_dim(value, length - width, length, axis=dim)
        leading = lax.slice_in_dim(value, 0, width, axis=dim)
        before = lax.ppermute(last, axis, up)
        after = lax.ppermute(leading, axis, down)
        value = jnp.concatenate([before, value, after], axis=dim)
    return value


def conv_valid(padded, kernel):
    return lax.conv_general_dilated(
        padded,
        kernel,
        (1, 1),
        ((0, 0), (1, 1)),
        dimension_numbers=("NHWC", "HWIO", "NHWC"),
        preferred_element_type=jnp.float32,
    )


def batch_norm(conv_out, interior, gain_row, shift_row, cell_total):
    first_moment, squares = lax.psum(
        (jnp.sum(interior, axis=(0, 1, 2)), jnp.sum(jnp.square(interior), axis=(0, 1, 2))),
        ("img", "row"),
    )
    average = first_moment / cell_total
    spread = squares / cell_total - average * average
    return (conv_out - average) * lax.rsqrt(spread + epsilon) * gain_row + shift_row


def rim_conv(source, kernel):
    padded = extended(source, (("row", 1),), 1)
    return conv_valid(padded, kernel)


def residual_unit(source, conv_weight, bn_gain, bn_bias, first, cell_total):
    conv_first = rim_conv(jax.nn.relu(source), conv_weight[first])
    hidden = jax.nn.relu(
        batch_norm(conv_first, conv_first, bn_gain[first], bn_bias[first], cell_total)
    ).astype(jnp.bfloat16)
    conv_second = rim_conv(hidden, conv_weight[first + 1])
    branch = batch_norm(
        conv_second, conv_second, bn_gain[first + 1], bn_bias[first + 1], cell_total
    )
    return source.astype(jnp.float32) + branch


def on_device(tokens, proj_weight, proj_bias, conv_weight, bn_gain, bn_bias):
    img_count, row_count, col_count, embed_dim = tokens.shape
    flat = (
        jnp.dot(tokens.reshape(-1, embed_dim), proj_weight, preferred_element_type=jnp.float32)
        + proj_bias
    )
    feature = flat.astype(jnp.bfloat16).reshape(img_count, row_count, col_count, -1)
    cell_total = float(
        lax.axis_size("img") * lax.axis_size("row") * img_count * row_count * col_count
    )
    joined = residual_unit(feature, conv_weight, bn_gain, bn_bias, 0, cell_total).astype(
        jnp.bfloat16
    )
    return residual_unit(joined, conv_weight, bn_gain, bn_bias, 2, cell_total).astype(jnp.bfloat16)


def solution(mesh):
    in_specs = (P("img", "row", None, None), P(), P(), P(), P(), P())
    out_specs = P("img", "row", None, None)
    return jax.shard_map(
        on_device, mesh=mesh, in_specs=in_specs, out_specs=out_specs, check_vma=False
    )
```

profile of v0, /device:TPU:0, one launch (start us, length us, event | category | flops | bytes accessed | tf_op | source)
XLA Modules:
  0.0 233.8 jit_solution(10061670409957228319)
XLA Ops:
  0.0 1.6 copy-done
  1.6 1.8 broadcast_maximum_fusion.1
  3.4 2.4 %collective-permute-start = (bf16[1,1,128,256]{3,2,1,0:T(8,128)(2,1)S(1)}, bf16[1,1,128,256]{3,2,1,0:T(8,128)(2,1)S(1)}, u32[]{:S(2)}, u32[]{:S(2)}) collective-permute-start(bf16[1,1,128,256]{3,2,1,0:T(8,128)(2,1)S(1)} %get-tuple-element.29), channel_id=1, source_target_pairs={{0,1},{1,2},{2,3},{4,5},{5,6},{6,7},{8,9},{9,10},{10,11},{12,13},{... | collective-permute-start | bytes 196616 | tf_op jit(solution)/shard_map/ppermute | solution.py:16
  5.8 1.3 collective-permute-start.1
  7.3 3.8 %collective-permute-done.1 = bf16[1,1,128,256]{3,2,1,0:T(8,128)(2,1)S(1)} collective-permute-done((bf16[1,1,128,256]{3,2,1,0:T(8,128)(2,1)S(1)}, bf16[1,1,128,256]{3,2,1,0:T(8,128)(2,1)S(1)}, u32[]{:S(2)}, u32[]{:S(2)}) %collective-permute-start.1) | collective-permute-done | bytes 65568 | tf_op jit(solution)/shard_map/ppermute | solution.py:17
  11.2 1.0 pad
  12.2 2.2 reshape.84
  14.4 1.4 copy.8
  15.8 3.7 %select_reduce_fusion.7 = (f32[256]{0:T(256)S(1)}, f32[256]{0:T(256)S(1)}, f32[8,8,17,256]{3,1,2,0:T(8,128)}) fusion(pred[8,17]{0,1:T(8,128)(4,1)S(1)} %copy-done.5, bf16[4,3,3,256,256]{4,3,2,1,0:T(8,128)(2,1)} %param.9, bf16[10,1,7,2,256]{4,2,3,0,1:T(8,128)(2,1)S(1)} %slice.98, bf16[10,1,8,17,256]{4,2,3,0,1:T(8,128)(2,1)S(1)} %copy.8), kind=kOutput, calls=%fused_computation.30 | convolution fusion | flops 1287462400 | bytes 3063944 | tf_op jit(solution)/shard_map/conv_general_dilated | solution.py:23
  19.5 41.9 %all-reduce.3 = (f32[256]{0:T(256)S(1)}, f32[256]{0:T(256)S(1)}) all-reduce(f32[256]{0:T(256)S(1)} %get-tuple-element.12, f32[256]{0:T(256)S(1)} %get-tuple-element.11), channel_id=1, replica_groups=mesh['img'=8,'row'=4] {'img','row'}, use_global_device_ids=true, to_apply=%region_3.4 | all-reduce | flops 512 | bytes 4096 | tf_op jit(solution)/shard_map/psum | solution.py:34
  61.4 1.5 maximum_convert_fusion.1
  64.5 1.3 collective-permute-start.2
  66.0 1.3 collective-permute-start.3
  67.3 1.1 slice_bitcast_fusion.3
  68.5 3.2 %collective-permute-done.3 = bf16[1,1,128,256]{3,1,2,0:T(2,128)(2,1)S(1)} collective-permute-done((bf16[1,1,128,256]{3,1,2,0:T(2,128)(2,1)S(1)}, bf16[1,1,128,256]{3,1,2,0:T(2,128)(2,1)S(1)}, u32[]{:S(2)}, u32[]{:S(2)}) %collective-permute-start.3) | collective-permute-done | bytes 65568 | tf_op jit(solution)/shard_map/ppermute | solution.py:17
  72.8 3.7 %select_reduce_fusion.5 = (f32[256]{0:T(256)S(1)}, f32[256]{0:T(256)S(1)}, f32[8,8,17,256]{3,1,2,0:T(8,128)}) fusion(pred[8,17]{0,1:T(8,128)(4,1)S(1)} %copy-done.5, bf16[4,3,3,256,256]{4,3,2,1,0:T(8,128)(2,1)} %param.9, bf16[10,1,7,2,256]{4,2,3,0,1:T(8,128)(2,1)S(1)} %slice.104, bf16[10,1,8,17,256]{4,2,3,0,1:T(8,128)(2,1)S(1)} %copy.16), kind=kOutput, calls=%fused_computation.27 | convolution fusion | flops 1287462400 | bytes 3063944 | tf_op jit(solution)/shard_map/conv_general_dilated | solution.py:23
  76.5 41.3 %all-reduce.2 = (f32[256]{0:T(256)S(1)}, f32[256]{0:T(256)S(1)}) all-reduce(f32[256]{0:T(256)S(1)} %get-tuple-element.10, f32[256]{0:T(256)S(1)} %get-tuple-element.9), channel_id=1, replica_groups=mesh['img'=8,'row'=4] {'img','row'}, use_global_device_ids=true, to_apply=%region_7.8 | all-reduce | flops 512 | bytes 4096 | tf_op jit(solution)/shard_map/psum | solution.py:34
  117.8 1.4 multiply_add_fusion.1
  119.6 1.5 broadcast_maximum_fusion
  121.2 1.3 collective-permute-start.4
  122.6 1.5 collective-permute-start.5
  124.0 4.2 %collective-permute-done.5 = bf16[1,1,128,256]{3,1,2,0:T(2,128)(2,1)S(1)} collective-permute-done((bf16[1,1,128,256]{3,1,2,0:T(2,128)(2,1)S(1)}, bf16[1,1,128,256]{3,1,2,0:T(2,128)(2,1)S(1)}, u32[]{:S(2)}, u32[]{:S(2)}) %collective-permute-start.5) | collective-permute-done | bytes 65568 | tf_op jit(solution)/shard_map/ppermute | solution.py:17
  129.4 3.7 %select_reduce_fusion.3 = (f32[256]{0:T(256)S(1)}, f32[256]{0:T(256)S(1)}, f32[8,8,17,256]{3,1,2,0:T(8,128)}) fusion(pred[8,17]{0,1:T(8,128)(4,1)S(1)} %copy-done.5, bf16[4,3,3,256,256]{4,3,2,1,0:T(8,128)(2,1)} %param.9, bf16[10,1,7,2,256]{4,2,3,0,1:T(8,128)(2,1)S(1)} %slice.108, bf16[10,1,8,17,256]{4,2,3,0,1:T(8,128)(2,1)S(1)} %copy.21), kind=kOutput, calls=%fused_computation.24 | convolution fusion | flops 1287462400 | bytes 3063944 | tf_op jit(solution)/shard_map/conv_general_dilated | solution.py:23
  133.1 41.1 %all-reduce.1 = (f32[256]{0:T(256)S(1)}, f32[256]{0:T(256)S(1)}) all-reduce(f32[256]{0:T(256)S(1)} %get-tuple-element.8, f32[256]{0:T(256)S(1)} %get-tuple-element.7), channel_id=1, replica_groups=mesh['img'=8,'row'=4] {'img','row'}, use_global_device_ids=true, to_apply=%region_11.12 | all-reduce | flops 512 | bytes 4096 | tf_op jit(solution)/shard_map/psum | solution.py:34
  174.3 1.5 maximum_convert_fusion
  175.8 0.9 copy.23
  176.7 1.4 collective-permute-start.6
  178.4 1.3 collective-permute-start.7
  179.9 4.3 %collective-permute-done.7 = bf16[1,1,128,256]{3,1,2,0:T(2,128)(2,1)S(1)} collective-permute-done((bf16[1,1,128,256]{3,1,2,0:T(2,128)(2,1)S(1)}, bf16[1,1,128,256]{3,1,2,0:T(2,128)(2,1)S(1)}, u32[]{:S(2)}, u32[]{:S(2)}) %collective-permute-start.7) | collective-permute-done | bytes 65568 | tf_op jit(solution)/shard_map/ppermute | solution.py:17
  185.2 3.7 %select_reduce_fusion.1 = (f32[256]{0:T(256)S(1)}, f32[256]{0:T(256)S(1)}, f32[8,8,17,256]{3,1,2,0:T(8,128)}) fusion(pred[8,17]{0,1:T(8,128)(4,1)S(1)} %copy-done.5, bf16[4,3,3,256,256]{4,3,2,1,0:T(8,128)(2,1)} %param.9, bf16[10,1,7,2,256]{4,2,3,0,1:T(8,128)(2,1)S(1)} %slice.114, bf16[10,1,8,17,256]{4,2,3,0,1:T(8,128)(2,1)S(1)} %copy.29), kind=kOutput, calls=%fused_computation.21 | convolution fusion | flops 1287462400 | bytes 3063944 | tf_op jit(solution)/shard_map/conv_general_dilated | solution.py:23
  189.0 41.4 %all-reduce = (f32[256]{0:T(256)S(1)}, f32[256]{0:T(256)S(1)}) all-reduce(f32[256]{0:T(256)S(1)} %get-tuple-element.6, f32[256]{0:T(256)S(1)} %get-tuple-element.5), channel_id=1, replica_groups=mesh['img'=8,'row'=4] {'img','row'}, use_global_device_ids=true, to_apply=%region_15.16 | all-reduce | flops 512 | bytes 4096 | tf_op jit(solution)/shard_map/psum | solution.py:34
  230.3 1.4 multiply_add_fusion
  (60 shorter events, 8.4 us)
Async XLA Ops:
  0.0 1.6 copy-start
  1.6 5.5 %copy-start.3 = (f32[4,256]{1,0:T(4,128)S(1)}, f32[4,256]{1,0:T(4,128)}, u32[]{:S(2)}) copy-start(f32[4,256]{1,0:T(4,128)} %param.10) | copy-start | bytes 12292
  1.6 5.5 %copy-start.4 = (f32[4,256]{1,0:T(4,128)S(1)}, f32[4,256]{1,0:T(4,128)}, u32[]{:S(2)}) copy-start(f32[4,256]{1,0:T(4,128)} %param.11) | copy-start | bytes 12292
  3.4 3.9 %collective-permute-start = (bf16[1,1,128,256]{3,2,1,0:T(8,128)(2,1)S(1)}, bf16[1,1,128,256]{3,2,1,0:T(8,128)(2,1)S(1)}, u32[]{:S(2)}, u32[]{:S(2)}) collective-permute-start(bf16[1,1,128,256]{3,2,1,0:T(8,128)(2,1)S(1)} %get-tuple-element.29), channel_id=1, source_target_pairs={{0,1},{1,2},{2,3},{4,5},{5,6},{6,7},{8,9},{9,10},{10,11},{12,13},{... | collective-permute-start | bytes 196616 | tf_op jit(solution)/shard_map/ppermute | solution.py:16
  5.8 5.3 %collective-permute-start.1 = (bf16[1,1,128,256]{3,2,1,0:T(8,128)(2,1)S(1)}, bf16[1,1,128,256]{3,2,1,0:T(8,128)(2,1)S(1)}, u32[]{:S(2)}, u32[]{:S(2)}) collective-permute-start(bf16[1,1,128,256]{3,2,1,0:T(8,128)(2,1)S(1)} %get-tuple-element.30), channel_id=1, source_target_pairs={{1,0},{2,1},{3,2},{5,4},{6,5},{7,6},{9,8},{10,9},{11,10},{13,12},{... | collective-permute-start | bytes 196616 | tf_op jit(solution)/shard_map/ppermute | solution.py:17
  14.4 1.4 copy-start.5
  64.5 3.9 %collective-permute-start.2 = (bf16[1,1,128,256]{3,2,1,0:T(8,128)(2,1)}, bf16[1,1,128,256]{3,2,1,0:T(8,128)(2,1)S(1)}, u32[]{:S(2)}, u32[]{:S(2)}) collective-permute-start(bf16[1,1,128,256]{3,2,1,0:T(8,128)(2,1)} %slice.100), channel_id=1, source_target_pairs={{0,1},{1,2},{2,3},{4,5},{5,6},{6,7},{8,9},{9,10},{10,11},{12,13},{... | collective-permute-start | bytes 196616 | tf_op jit(solution)/shard_map/ppermute | solution.py:16
  66.0 5.7 %collective-permute-start.3 = (bf16[1,1,128,256]{3,1,2,0:T(2,128)(2,1)S(1)}, bf16[1,1,128,256]{3,1,2,0:T(2,128)(2,1)S(1)}, u32[]{:S(2)}, u32[]{:S(2)}) collective-permute-start(bf16[1,1,128,256]{3,1,2,0:T(2,128)(2,1)S(1)} %slice.103), channel_id=1, source_target_pairs={{1,0},{2,1},{3,2},{5,4},{6,5},{7,6},{9,8},{10,9},{11,10},{13,12},{... | collective-permute-start | bytes 196616 | tf_op jit(solution)/shard_map/ppermute | solution.py:17
  121.2 2.8 %collective-permute-start.4 = (bf16[1,1,128,256]{3,1,2,0:T(2,128)(2,1)S(1)}, bf16[1,1,128,256]{3,1,2,0:T(2,128)(2,1)S(1)}, u32[]{:S(2)}, u32[]{:S(2)}) collective-permute-start(bf16[1,1,128,256]{3,1,2,0:T(2,128)(2,1)S(1)} %get-tuple-element.27), channel_id=1, source_target_pairs={{0,1},{1,2},{2,3},{4,5},{5,6},{6,7},{8,9},{9,10},{10,11},{12,13},{... | collective-permute-start | bytes 196616 | tf_op jit(solution)/shard_map/ppermute | solution.py:16
  122.6 5.7 %collective-permute-start.5 = (bf16[1,1,128,256]{3,1,2,0:T(2,128)(2,1)S(1)}, bf16[1,1,128,256]{3,1,2,0:T(2,128)(2,1)S(1)}, u32[]{:S(2)}, u32[]{:S(2)}) collective-permute-start(bf16[1,1,128,256]{3,1,2,0:T(2,128)(2,1)S(1)} %get-tuple-element.28), channel_id=1, source_target_pairs={{1,0},{2,1},{3,2},{5,4},{6,5},{7,6},{9,8},{10,9},{11,10},{13,12},{... | collective-permute-start | bytes 196616 | tf_op jit(solution)/shard_map/ppermute | solution.py:17
  176.7 3.0 %copy-start.1 = (bf16[8,8,17,256]{3,0,2,1:T(8,128)(2,1)S(1)}, bf16[8,8,17,256]{3,0,2,1:T(8,128)(2,1)}, u32[]{:S(2)}) copy-start(bf16[8,8,17,256]{3,0,2,1:T(8,128)(2,1)} %copy.23) | copy-start | bytes 1671172
  176.7 3.0 %collective-permute-start.6 = (bf16[1,1,128,256]{3,2,1,0:T(8,128)(2,1)S(1)}, bf16[1,1,128,256]{3,2,1,0:T(8,128)(2,1)S(1)}, u32[]{:S(2)}, u32[]{:S(2)}) collective-permute-start(bf16[1,1,128,256]{3,2,1,0:T(8,128)(2,1)S(1)} %slice.110), channel_id=1, source_target_pairs={{0,1},{1,2},{2,3},{4,5},{5,6},{6,7},{8,9},{9,10},{10,11},{12,13},{... | collective-permute-start | bytes 196616 | tf_op jit(solution)/shard_map/ppermute | solution.py:16
  178.4 5.7 %collective-permute-start.7 = (bf16[1,1,128,256]{3,1,2,0:T(2,128)(2,1)S(1)}, bf16[1,1,128,256]{3,1,2,0:T(2,128)(2,1)S(1)}, u32[]{:S(2)}, u32[]{:S(2)}) collective-permute-start(bf16[1,1,128,256]{3,1,2,0:T(2,128)(2,1)S(1)} %slice.113), channel_id=1, source_target_pairs={{1,0},{2,1},{3,2},{5,4},{6,5},{7,6},{9,8},{10,9},{11,10},{13,12},{... | collective-permute-start | bytes 196616 | tf_op jit(solution)/shard_map/ppermute | solution.py:17
  231.8 1.0 copy-start.2
where the time goes:
time: 235 us; the launch traced here: 234 us
  blocking collectives  166 us (71%)
  matrix products  16.7 us (7%)
  waiting for transfers between devices  15.6 us (7%)
  local copies, waits for them, and re-layouts  14.1 us (6%)
  starting transfers between devices  11.8 us (5%)
  other arithmetic  9.63 us (4%)
    psum x4, blocking collectives, batch_norm(): lax.psum((jnp.sum(interior, axis=(0, 1, 2)), jnp.sum(jnp.square(interior)...  166 us
    ppermute x4, waiting for transfers between devices, extended(): after = lax.ppermute(leading, axis, down)  15.6 us
    conv_general_dilated x4, matrix products, conv_valid(): lax.conv_general_dilated(padded, kernel, (1, 1), ((0, 0), (1, 1)), dimens...  15 us
    ppermute x4, starting transfers between devices, extended(): before = lax.ppermute(last, axis, up)  6.4 us
    ppermute x4, starting transfers between devices, extended(): after = lax.ppermute(leading, axis, down)  5.35 us
  transfers between devices with their start and end apart: 8, of which 4 were waited for; matrix products, arithmetic and copies ran while one was open for 1% of the time, Pallas kernels for 0%

commit v1 on v0

--- a/solution.py
+++ b/solution.py
@@ -32,8 +32,11 @@
 
 def batch_norm(conv_out, interior, gain_row, shift_row, cell_total):
     first_moment, squares = lax.psum(
-        (jnp.sum(interior, axis=(0, 1, 2)), jnp.sum(jnp.square(interior), axis=(0, 1, 2))),
-        ("img", "row"),
+        lax.psum(
+            (jnp.sum(interior, axis=(0, 1, 2)), jnp.sum(jnp.square(interior), axis=(0, 1, 2))),
+            "row",
+        ),
+        "img",
     )
     average = first_moment / cell_total
     spread = squares / cell_total - average * average

time: 235 us -> 178 us (0.76)
  blocking collectives: 166 us -> 111 us
    psum x4, blocking collectives: 166 us -> 36.1 us  [batch_norm(): lax.psum((jnp.sum(interior, axis=(0, 1, 2)), jnp.sum(jnp.square(interior)...]
    psum x0 -> x4, blocking collectives: none -> 75 us  [batch_norm(): lax.psum(lax.psum((jnp.sum(interior, axis=(0, 1, 2)), jnp.sum(jnp.square(...]
where the time goes in v1:
time: 178 us
  blocking collectives  111 us (62%)
  matrix products  16.7 us (9%)
  local copies, waits for them, and re-layouts  14.1 us (8%)
  waiting for transfers between devices  13.9 us (8%)
  starting transfers between devices  11.8 us (7%)
  other arithmetic  9.64 us (5%)
    psum x4, blocking collectives, batch_norm(): lax.psum(lax.psum((jnp.sum(interior, axis=(0, 1, 2)), jnp.sum(jnp.square(...  75 us
    psum x4, blocking collectives, batch_norm(): lax.psum((jnp.sum(interior, axis=(0, 1, 2)), jnp.sum(jnp.square(interior)...  36.1 us
    conv_general_dilated x4, matrix products, conv_valid(): lax.conv_general_dilated(padded, kernel, (1, 1), ((0, 0), (1, 1)), dimens...  15 us
    ppermute x4, waiting for transfers between devices, extended(): after = lax.ppermute(leading, axis, down)  13.9 us
    ppermute x4, starting transfers between devices, extended(): before = lax.ppermute(last, axis, up)  6.58 us
    ppermute x4, starting transfers between devices, extended(): after = lax.ppermute(leading, axis, down)  5.17 us
    conv_general_dilated x9, local copies, waits for them, and re-layouts, conv_valid(): lax.conv_general_dilated(padded, kernel, (1, 1), ((0, 0), (1, 1)), dimens...  4.28 us
    convert_element_type x18, local copies, waits for them, and re-layouts, residual_unit(): hidden = jax.nn.relu(batch_norm(conv_first, conv_first, bn_gain[first], b...  4.1 us
  transfers between devices with their start and end apart: 8, of which 4 were waited for; matrix products, arithmetic and copies ran while one was open for 1% of the time, Pallas kernels for 0%

profile of v1, /device:TPU:0, one launch (start us, length us, event | category | flops | bytes accessed | tf_op | source)
XLA Modules:
  0.0 177.5 jit_solution(4226577254949426317)
XLA Ops:
  0.0 1.6 copy-done
  1.6 1.8 %broadcast_maximum_fusion.1 = (bf16[1024,256]{1,0:T(8,128)(2,1)S(1)}, bf16[1024,256]{1,0:T(8,128)(2,1)S(1)}) fusion(f32[256]{0:T(256)} %param.8, bf16[1024,1024]{1,0:T(8,128)(2,1)S(1)} %bitcast.90, bf16[1024,256]{1,0:T(8,128)(2,1)} %param.7), kind=kOutput, calls=%fused_computation.68 | convolution fusion | flops 537657344 | bytes 3671040 | tf_op jit(solution)/shard_map/dot_general | solution.py:66
  3.4 2.4 %collective-permute-start = (bf16[1,1,128,256]{3,2,1,0:T(8,128)(2,1)S(1)}, bf16[1,1,128,256]{3,2,1,0:T(8,128)(2,1)S(1)}, u32[]{:S(2)}, u32[]{:S(2)}) collective-permute-start(bf16[1,1,128,256]{3,2,1,0:T(8,128)(2,1)S(1)} %get-tuple-element.37), channel_id=1, source_target_pairs={{0,1},{1,2},{2,3},{4,5},{5,6},{6,7},{8,9},{9,10},{10,11},{12,13},{... | collective-permute-start | bytes 196616 | tf_op jit(solution)/shard_map/ppermute | solution.py:16
  5.8 1.3 collective-permute-start.1
  7.3 3.8 %collective-permute-done.1 = bf16[1,1,128,256]{3,2,1,0:T(8,128)(2,1)S(1)} collective-permute-done((bf16[1,1,128,256]{3,2,1,0:T(8,128)(2,1)S(1)}, bf16[1,1,128,256]{3,2,1,0:T(8,128)(2,1)S(1)}, u32[]{:S(2)}, u32[]{:S(2)}) %collective-permute-start.1) | collective-permute-done | bytes 65568 | tf_op jit(solution)/shard_map/ppermute | solution.py:17
  12.2 2.2 %reshape.84 = bf16[10,1,8,17,256]{4,3,2,0,1:T(8,128)(2,1)} reshape(bf16[10,1,136,256]{3,2,0,1:T(8,128)(2,1)} %pad) | data formatting | bytes 1392640 | tf_op jit(solution)/shard_map/conv_general_dilated | solution.py:23
  14.4 1.4 copy.8
  15.8 3.7 %select_reduce_fusion.7 = (f32[256]{0:T(256)S(1)}, f32[256]{0:T(256)S(1)}, f32[8,8,17,256]{3,1,2,0:T(8,128)}) fusion(pred[8,17]{0,1:T(8,128)(4,1)S(1)} %copy-done.5, bf16[4,3,3,256,256]{4,3,2,1,0:T(8,128)(2,1)} %param.9, bf16[10,1,7,2,256]{4,2,3,0,1:T(8,128)(2,1)S(1)} %slice.98, bf16[10,1,8,17,256]{4,2,3,0,1:T(8,128)(2,1)S(1)} %copy.8), kind=kOutput, calls=%fused_computation.30 | convolution fusion | flops 1287462400 | bytes 3063944 | tf_op jit(solution)/shard_map/conv_general_dilated | solution.py:23
  19.5 8.6 %all-reduce.7 = (f32[256]{0:T(256)S(1)}, f32[256]{0:T(256)S(1)}) all-reduce(f32[256]{0:T(256)S(1)} %get-tuple-element.12, f32[256]{0:T(256)S(1)} %get-tuple-element.11), channel_id=1, replica_groups=mesh['img'=8,'row'=4] {'row'}, use_global_device_ids=true, to_apply=%region_4.5 | all-reduce | flops 512 | bytes 4096 | tf_op jit(solution)/shard_map/psum | solution.py:35
  28.1 21.6 %all-reduce.3 = (f32[256]{0:T(256)S(1)}, f32[256]{0:T(256)S(1)}) all-reduce(f32[256]{0:T(256)S(1)} %get-tuple-element.27, f32[256]{0:T(256)S(1)} %get-tuple-element.28), channel_id=1, replica_groups=mesh['img'=8,'row'=4] {'img'}, use_global_device_ids=true, to_apply=%region_5.6 | all-reduce | flops 512 | bytes 4096 | tf_op jit(solution)/shard_map/psum | solution.py:34
  49.7 1.5 maximum_convert_fusion.1
  54.3 1.3 collective-permute-start.3
  56.8 2.6 %collective-permute-done.3 = bf16[1,1,128,256]{3,1,2,0:T(2,128)(2,1)S(1)} collective-permute-done((bf16[1,1,128,256]{3,1,2,0:T(2,128)(2,1)S(1)}, bf16[1,1,128,256]{3,1,2,0:T(2,128)(2,1)S(1)}, u32[]{:S(2)}, u32[]{:S(2)}) %collective-permute-start.3) | collective-permute-done | bytes 65568 | tf_op jit(solution)/shard_map/ppermute | solution.py:17
  60.5 3.7 %select_reduce_fusion.5 = (f32[256]{0:T(256)S(1)}, f32[256]{0:T(256)S(1)}, f32[8,8,17,256]{3,1,2,0:T(8,128)}) fusion(pred[8,17]{0,1:T(8,128)(4,1)S(1)} %copy-done.5, bf16[4,3,3,256,256]{4,3,2,1,0:T(8,128)(2,1)} %param.9, bf16[10,1,7,2,256]{4,2,3,0,1:T(8,128)(2,1)S(1)} %slice.104, bf16[10,1,8,17,256]{4,2,3,0,1:T(8,128)(2,1)S(1)} %copy.16), kind=kOutput, calls=%fused_computation.27 | convolution fusion | flops 1287462400 | bytes 3063944 | tf_op jit(solution)/shard_map/conv_general_dilated | solution.py:23
  64.2 9.2 %all-reduce.6 = (f32[256]{0:T(256)S(1)}, f32[256]{0:T(256)S(1)}) all-reduce(f32[256]{0:T(256)S(1)} %get-tuple-element.10, f32[256]{0:T(256)S(1)} %get-tuple-element.9), channel_id=1, replica_groups=mesh['img'=8,'row'=4] {'row'}, use_global_device_ids=true, to_apply=%region_10.11 | all-reduce | flops 512 | bytes 4096 | tf_op jit(solution)/shard_map/psum | solution.py:35
  73.4 17.1 %all-reduce.2 = (f32[256]{0:T(256)S(1)}, f32[256]{0:T(256)S(1)}) all-reduce(f32[256]{0:T(256)S(1)} %get-tuple-element.25, f32[256]{0:T(256)S(1)} %get-tuple-element.26), channel_id=1, replica_groups=mesh['img'=8,'row'=4] {'img'}, use_global_device_ids=true, to_apply=%region_11.12 | all-reduce | flops 512 | bytes 4096 | tf_op jit(solution)/shard_map/psum | solution.py:34
  90.5 1.4 multiply_add_fusion.1
  92.3 1.5 broadcast_maximum_fusion
  93.9 1.3 collective-permute-start.4
  95.3 1.3 collective-permute-start.5
  96.6 3.8 %collective-permute-done.5 = bf16[1,1,128,256]{3,1,2,0:T(2,128)(2,1)S(1)} collective-permute-done((bf16[1,1,128,256]{3,1,2,0:T(2,128)(2,1)S(1)}, bf16[1,1,128,256]{3,1,2,0:T(2,128)(2,1)S(1)}, u32[]{:S(2)}, u32[]{:S(2)}) %collective-permute-start.5) | collective-permute-done | bytes 65568 | tf_op jit(solution)/shard_map/ppermute | solution.py:17
  101.5 3.7 %select_reduce_fusion.3 = (f32[256]{0:T(256)S(1)}, f32[256]{0:T(256)S(1)}, f32[8,8,17,256]{3,1,2,0:T(8,128)}) fusion(pred[8,17]{0,1:T(8,128)(4,1)S(1)} %copy-done.5, bf16[4,3,3,256,256]{4,3,2,1,0:T(8,128)(2,1)} %param.9, bf16[10,1,7,2,256]{4,2,3,0,1:T(8,128)(2,1)S(1)} %slice.108, bf16[10,1,8,17,256]{4,2,3,0,1:T(8,128)(2,1)S(1)} %copy.21), kind=kOutput, calls=%fused_computation.24 | convolution fusion | flops 1287462400 | bytes 3063944 | tf_op jit(solution)/shard_map/conv_general_dilated | solution.py:23
  105.2 9.2 %all-reduce.5 = (f32[256]{0:T(256)S(1)}, f32[256]{0:T(256)S(1)}) all-reduce(f32[256]{0:T(256)S(1)} %get-tuple-element.8, f32[256]{0:T(256)S(1)} %get-tuple-element.7), channel_id=1, replica_groups=mesh['img'=8,'row'=4] {'row'}, use_global_device_ids=true, to_apply=%region_16.17 | all-reduce | flops 512 | bytes 4096 | tf_op jit(solution)/shard_map/psum | solution.py:35
  114.4 19.1 %all-reduce.1 = (f32[256]{0:T(256)S(1)}, f32[256]{0:T(256)S(1)}) all-reduce(f32[256]{0:T(256)S(1)} %get-tuple-element.23, f32[256]{0:T(256)S(1)} %get-tuple-element.24), channel_id=1, replica_groups=mesh['img'=8,'row'=4] {'img'}, use_global_device_ids=true, to_apply=%region_17.18 | all-reduce | flops 512 | bytes 4096 | tf_op jit(solution)/shard_map/psum | solution.py:34
  133.5 1.5 maximum_convert_fusion
  135.9 1.6 collective-permute-start.6
  137.8 1.3 collective-permute-start.7
  139.3 3.6 %collective-permute-done.7 = bf16[1,1,128,256]{3,1,2,0:T(2,128)(2,1)S(1)} collective-permute-done((bf16[1,1,128,256]{3,1,2,0:T(2,128)(2,1)S(1)}, bf16[1,1,128,256]{3,1,2,0:T(2,128)(2,1)S(1)}, u32[]{:S(2)}, u32[]{:S(2)}) %collective-permute-start.7) | collective-permute-done | bytes 65568 | tf_op jit(solution)/shard_map/ppermute | solution.py:17
  144.0 3.7 %select_reduce_fusion.1 = (f32[256]{0:T(256)S(1)}, f32[256]{0:T(256)S(1)}, f32[8,8,17,256]{3,1,2,0:T(8,128)}) fusion(pred[8,17]{0,1:T(8,128)(4,1)S(1)} %copy-done.5, bf16[4,3,3,256,256]{4,3,2,1,0:T(8,128)(2,1)} %param.9, bf16[10,1,7,2,256]{4,2,3,0,1:T(8,128)(2,1)S(1)} %slice.114, bf16[10,1,8,17,256]{4,2,3,0,1:T(8,128)(2,1)S(1)} %copy.29), kind=kOutput, calls=%fused_computation.21 | convolution fusion | flops 1287462400 | bytes 3063944 | tf_op jit(solution)/shard_map/conv_general_dilated | solution.py:23
  147.7 9.2 %all-reduce.4 = (f32[256]{0:T(256)S(1)}, f32[256]{0:T(256)S(1)}) all-reduce(f32[256]{0:T(256)S(1)} %get-tuple-element.6, f32[256]{0:T(256)S(1)} %get-tuple-element.5), channel_id=1, replica_groups=mesh['img'=8,'row'=4] {'row'}, use_global_device_ids=true, to_apply=%region_22.23 | all-reduce | flops 512 | bytes 4096 | tf_op jit(solution)/shard_map/psum | solution.py:35
  156.9 17.2 %all-reduce = (f32[256]{0:T(256)S(1)}, f32[256]{0:T(256)S(1)}) all-reduce(f32[256]{0:T(256)S(1)} %get-tuple-element.21, f32[256]{0:T(256)S(1)} %get-tuple-element.22), channel_id=1, replica_groups=mesh['img'=8,'row'=4] {'img'}, use_global_device_ids=true, to_apply=%region_23.24 | all-reduce | flops 512 | bytes 4096 | tf_op jit(solution)/shard_map/psum | solution.py:34
  174.0 1.4 multiply_add_fusion
  (64 shorter events, 12.7 us)
Async XLA Ops:
  0.0 1.6 copy-start
  1.6 5.5 %copy-start.3 = (f32[4,256]{1,0:T(4,128)S(1)}, f32[4,256]{1,0:T(4,128)}, u32[]{:S(2)}) copy-start(f32[4,256]{1,0:T(4,128)} %param.10) | copy-start | bytes 12292
  1.6 5.5 %copy-start.4 = (f32[4,256]{1,0:T(4,128)S(1)}, f32[4,256]{1,0:T(4,128)}, u32[]{:S(2)}) copy-start(f32[4,256]{1,0:T(4,128)} %param.11) | copy-start | bytes 12292
  3.4 3.9 %collective-permute-start = (bf16[1,1,128,256]{3,2,1,0:T(8,128)(2,1)S(1)}, bf16[1,1,128,256]{3,2,1,0:T(8,128)(2,1)S(1)}, u32[]{:S(2)}, u32[]{:S(2)}) collective-permute-start(bf16[1,1,128,256]{3,2,1,0:T(8,128)(2,1)S(1)} %get-tuple-element.37), channel_id=1, source_target_pairs={{0,1},{1,2},{2,3},{4,5},{5,6},{6,7},{8,9},{9,10},{10,11},{12,13},{... | collective-permute-start | bytes 196616 | tf_op jit(solution)/shard_map/ppermute | solution.py:16
  5.8 5.3 %collective-permute-start.1 = (bf16[1,1,128,256]{3,2,1,0:T(8,128)(2,1)S(1)}, bf16[1,1,128,256]{3,2,1,0:T(8,128)(2,1)S(1)}, u32[]{:S(2)}, u32[]{:S(2)}) collective-permute-start(bf16[1,1,128,256]{3,2,1,0:T(8,128)(2,1)S(1)} %get-tuple-element.38), channel_id=1, source_target_pairs={{1,0},{2,1},{3,2},{5,4},{6,5},{7,6},{9,8},{10,9},{11,10},{13,12},{... | collective-permute-start | bytes 196616 | tf_op jit(solution)/shard_map/ppermute | solution.py:17
  14.4 1.4 copy-start.5
  52.8 3.9 %collective-permute-start.2 = (bf16[1,1,128,256]{3,2,1,0:T(8,128)(2,1)}, bf16[1,1,128,256]{3,2,1,0:T(8,128)(2,1)S(1)}, u32[]{:S(2)}, u32[]{:S(2)}) collective-permute-start(bf16[1,1,128,256]{3,2,1,0:T(8,128)(2,1)} %slice.100), channel_id=1, source_target_pairs={{0,1},{1,2},{2,3},{4,5},{5,6},{6,7},{8,9},{9,10},{10,11},{12,13},{... | collective-permute-start | bytes 196616 | tf_op jit(solution)/shard_map/ppermute | solution.py:16
  54.3 5.1 %collective-permute-start.3 = (bf16[1,1,128,256]{3,1,2,0:T(2,128)(2,1)S(1)}, bf16[1,1,128,256]{3,1,2,0:T(2,128)(2,1)S(1)}, u32[]{:S(2)}, u32[]{:S(2)}) collective-permute-start(bf16[1,1,128,256]{3,1,2,0:T(2,128)(2,1)S(1)} %slice.103), channel_id=1, source_target_pairs={{1,0},{2,1},{3,2},{5,4},{6,5},{7,6},{9,8},{10,9},{11,10},{13,12},{... | collective-permute-start | bytes 196616 | tf_op jit(solution)/shard_map/ppermute | solution.py:17
  93.9 2.6 %collective-permute-start.4 = (bf16[1,1,128,256]{3,1,2,0:T(2,128)(2,1)S(1)}, bf16[1,1,128,256]{3,1,2,0:T(2,128)(2,1)S(1)}, u32[]{:S(2)}, u32[]{:S(2)}) collective-permute-start(bf16[1,1,128,256]{3,1,2,0:T(2,128)(2,1)S(1)} %get-tuple-element.35), channel_id=1, source_target_pairs={{0,1},{1,2},{2,3},{4,5},{5,6},{6,7},{8,9},{9,10},{10,11},{12,13},{... | collective-permute-start | bytes 196616 | tf_op jit(solution)/shard_map/ppermute | solution.py:16
  95.3 5.1 %collective-permute-start.5 = (bf16[1,1,128,256]{3,1,2,0:T(2,128)(2,1)S(1)}, bf16[1,1,128,256]{3,1,2,0:T(2,128)(2,1)S(1)}, u32[]{:S(2)}, u32[]{:S(2)}) collective-permute-start(bf16[1,1,128,256]{3,1,2,0:T(2,128)(2,1)S(1)} %get-tuple-element.36), channel_id=1, source_target_pairs={{1,0},{2,1},{3,2},{5,4},{6,5},{7,6},{9,8},{10,9},{11,10},{13,12},{... | collective-permute-start | bytes 196616 | tf_op jit(solution)/shard_map/ppermute | solution.py:17
  135.9 3.2 %copy-start.1 = (bf16[8,8,17,256]{3,0,2,1:T(8,128)(2,1)S(1)}, bf16[8,8,17,256]{3,0,2,1:T(8,128)(2,1)}, u32[]{:S(2)}) copy-start(bf16[8,8,17,256]{3,0,2,1:T(8,128)(2,1)} %copy.23) | copy-start | bytes 1671172
  135.9 3.2 %collective-permute-start.6 = (bf16[1,1,128,256]{3,2,1,0:T(8,128)(2,1)S(1)}, bf16[1,1,128,256]{3,2,1,0:T(8,128)(2,1)S(1)}, u32[]{:S(2)}, u32[]{:S(2)}) collective-permute-start(bf16[1,1,128,256]{3,2,1,0:T(8,128)(2,1)S(1)} %slice.110), channel_id=1, source_target_pairs={{0,1},{1,2},{2,3},{4,5},{5,6},{6,7},{8,9},{9,10},{10,11},{12,13},{... | collective-permute-start | bytes 196616 | tf_op jit(solution)/shard_map/ppermute | solution.py:16
  137.8 5.1 %collective-permute-start.7 = (bf16[1,1,128,256]{3,1,2,0:T(2,128)(2,1)S(1)}, bf16[1,1,128,256]{3,1,2,0:T(2,128)(2,1)S(1)}, u32[]{:S(2)}, u32[]{:S(2)}) collective-permute-start(bf16[1,1,128,256]{3,1,2,0:T(2,128)(2,1)S(1)} %slice.113), channel_id=1, source_target_pairs={{1,0},{2,1},{3,2},{5,4},{6,5},{7,6},{9,8},{10,9},{11,10},{13,12},{... | collective-permute-start | bytes 196616 | tf_op jit(solution)/shard_map/ppermute | solution.py:17
  175.5 1.0 copy-start.2
